TPU v7x, 32 devices: a whole 2x2x4 slice. The times are simulated.
32 devices in a mesh: rows: 2 (over y), cols: 4 (over z), slabs: 2 (over x), trial: 2 (over core).
Axes of the slice: x: 2, y: 2, z: 4, core: 2. Of those that a mesh axis runs over, the one named last changes fastest.
Arguments:
- field_values: float32 [64, 16, 256, 128], P(('trial', 'rows'), 'cols', 'slabs'), parts along dimension 0, may hold values from 0.5 to 2
- conductance: float32 [64, 16, 256, 128], P(('trial', 'rows'), 'cols', 'slabs'), parts along dimension 0, may hold values from 0.03 to 0.15
- source: float32 [64, 16, 256, 128], P(('trial', 'rows'), 'cols', 'slabs'), parts along dimension 0, may hold values from -0.2 to 0.2
Outputs:
- anomaly: float32 [64, 16, 256, 128], P(('trial', 'rows'), 'cols', 'slabs'), parts along dimension 0
- field_values_end: float32 [64, 16, 256, 128], P(('trial', 'rows'), 'cols', 'slabs'), parts along dimension 0
There are 2 independent parts, one for each index of `trial`. A program takes and returns all parts, laid end to end along the dimension named above; each array names one. Nothing has to cross between parts.
All inputs are finite; a program needn't handle non-finite values.
Results may differ from a plain program's by a relative error of at most 0.00002.
Values sent between devices are 32-bit elements; how exact they have to be, the bound alone decides.
A program may use at most 128 MiB of HBM per device.

v0:
```python
import jax
import jax.numpy as jnp
from jax import lax
from jax.sharding import PartitionSpec as P

STEPS = 4


def extended(cells, sides, width):
    for axis, dim in sides:
        count = lax.axis_size(axis)
        ends = count - 1
        head = lax.slice_in_dim(cells, 0, width, axis=dim)
        tail = lax.slice_in_dim(cells, cells.shape[dim] - width, cells.shape[dim], axis=dim)
        cells = jnp.concatenate(
            [
                lax.ppermute(tail, axis, [(i, (i + 1) % count) for i in range(ends)]),
                cells,
                lax.ppermute(head, axis, [((i + 1) % count, i) for i in range(ends)]),
            ],
            axis=dim,
        )
    return cells


def strip_edges(values, dims):
    for dim in dims:
        values = lax.slice_in_dim(values, 1, values.shape[dim] - 1, axis=dim)
    return values


def neighbour(values, dim, start, dims):
    others = [other for other in dims if other != dim]
    values = strip_edges(values, others)
    return lax.slice_in_dim(values, start, start + values.shape[dim] - 2, axis=dim)


def one_step(padded, conductance, source):
    middle = strip_edges(padded, (0, 1, 2))
    lower = [neighbour(padded, dim, 0, (0, 1, 2)) for dim in (0, 1, 2)]
    upper = [neighbour(padded, dim, 2, (0, 1, 2)) for dim in (0, 1, 2)]
    spread = lower[0] + upper[0] + lower[1] + upper[1] + lower[2] + upper[2] - 6.0 * middle
    return middle + conductance * spread + source


def on_device(field_values, conductance, source):
    for step in range(STEPS):
        padded = extended(field_values, (("rows", 0), ("cols", 1), ("slabs", 2)), 1)
        field_values = one_step(padded, conductance, source)
    count = field_values.shape[0] * lax.axis_size("rows")
    guess = 1.0
    moved = field_values - guess
    totals, squares = lax.psum(
        (jnp.sum(moved, axis=0, keepdims=True), jnp.sum(moved * moved, axis=0, keepdims=True)),
        "rows",
    )
    line_mean = guess + totals / count
    centred = field_values - line_mean
    line_variance = squares / count - totals / count * (totals / count)
    anomaly = centred * lax.rsqrt(line_variance + 0.0001)
    return (anomaly, field_values)


def solution(mesh):
    in_specs = (
        P(("trial", "rows"), "cols", "slabs", None),
        P(("trial", "rows"), "cols", "slabs", None),
        P(("trial", "rows"), "cols", "slabs", None),
    )
    out_specs = (
        P(("trial", "rows"), "cols", "slabs", None),
        P(("trial", "rows"), "cols", "slabs", None),
    )
    return jax.shard_map(
        on_device, mesh=mesh, in_specs=in_specs, out_specs=out_specs, check_vma=False
    )
```

profile of v0, /device:TPU:0, one launch (start us, length us, event | category | flops | bytes accessed | tf_op | source)
XLA Modules:
  0.0 269.4 jit_solution(2563802980039127332)
XLA Ops:
  8.3 4.9 %collective-permute-start = (f32[1,4,128,128]{3,2,1,0:T(8,128)S(1)}, f32[1,4,128,128]{3,2,1,0:T(8,128)S(1)}, u32[]{:S(2)}, u32[]{:S(2)}) collective-permute-start(f32[1,4,128,128]{3,2,1,0:T(8,128)S(1)} %get-tuple-element.30), channel_id=1, source_target_pairs={{0,16},{1,17},{2,18},{3,19},{4,20},{5,21},{6,22},{7,23},{8,24},{9,... | collective-permute-start | bytes 786440 | tf_op jit(solution)/shard_map/ppermute | solution.py:17
  14.5 4.2 %collective-permute-done = f32[1,4,128,128]{3,2,1,0:T(8,128)S(1)} collective-permute-done((f32[1,4,128,128]{3,2,1,0:T(8,128)S(1)}, f32[1,4,128,128]{3,2,1,0:T(8,128)S(1)}, u32[]{:S(2)}, u32[]{:S(2)}) %collective-permute-start) | collective-permute-done | bytes 262176 | tf_op jit(solution)/shard_map/ppermute | solution.py:17
  23.1 3.6 %collective-permute-start.2 = (f32[18,1,128,128]{3,2,1,0:T(8,128)S(1)}, f32[18,1,128,128]{3,2,1,0:T(8,128)S(1)}, u32[]{:S(2)}, u32[]{:S(2)}) collective-permute-start(f32[18,1,128,128]{3,2,1,0:T(8,128)S(1)} %get-tuple-element.21), channel_id=1, source_target_pairs={{0,4},{4,8},{8,12},{1,5},{5,9},{9,13},{2,6},{6,10},{10,14},{3,7},{... | collective-permute-start | bytes 3538952 | tf_op jit(solution)/shard_map/ppermute | solution.py:17
  28.0 22.7 %collective-permute-done.2 = f32[18,1,128,128]{3,2,1,0:T(8,128)S(1)} collective-permute-done((f32[18,1,128,128]{3,2,1,0:T(8,128)S(1)}, f32[18,1,128,128]{3,2,1,0:T(8,128)S(1)}, u32[]{:S(2)}, u32[]{:S(2)}) %collective-permute-start.2) | collective-permute-done | bytes 1179680 | tf_op jit(solution)/shard_map/ppermute | solution.py:17
  50.7 4.2 %collective-permute-done.3 = f32[18,1,128,128]{3,2,1,0:T(8,128)S(1)} collective-permute-done((f32[18,1,128,128]{3,2,1,0:T(8,128)S(1)}, f32[18,1,128,128]{3,2,1,0:T(8,128)S(1)}, u32[]{:S(2)}, u32[]{:S(2)}) %collective-permute-start.3) | collective-permute-done | bytes 1179680 | tf_op jit(solution)/shard_map/ppermute | solution.py:19
  55.0 3.4 %collective-permute-start.4 = (f32[18,6,1,128]{3,2,1,0:T(1,128)S(1)}, f32[18,6,1,128]{3,2,1,0:T(1,128)S(1)}, u32[]{:S(2)}, u32[]{:S(2)}) collective-permute-start(f32[18,6,1,128]{3,2,1,0:T(1,128)S(1)} %get-tuple-element.13), channel_id=1, source_target_pairs={{0,2},{1,3},{4,6},{5,7},{8,10},{9,11},{12,14},{13,15},{16,18},{17,... | collective-permute-start | bytes 165896 | tf_op jit(solution)/shard_map/ppermute | solution.py:17
  60.2 4.3 %collective-permute-done.5 = f32[18,6,1,128]{3,2,1,0:T(1,128)S(1)} collective-permute-done((f32[18,6,1,128]{3,2,1,0:T(1,128)S(1)}, f32[18,6,1,128]{3,2,1,0:T(1,128)S(1)}, u32[]{:S(2)}, u32[]{:S(2)}) %collective-permute-start.5) | collective-permute-done | bytes 55328 | tf_op jit(solution)/shard_map/ppermute | solution.py:19
  64.4 18.6 %fusion.31 = f32[16,4,128,128]{3,2,1,0:T(8,128)S(1)} fusion(f32[16,4,128,128]{3,2,1,0:T(8,128)} %param.5, f32[16,4,128,128]{3,2,1,0:T(8,128)} %param.3, f32[16,4,128,128]{3,2,1,0:T(8,128)} %param.4, f32[18,6,1,128]{3,2,1,0:T(1,128)S(1)} %collective-permute-done.5, f32[18,1,128,128]{3,2,1,0:T(8,128)S(1)} %collective-permute-done.3, ...), kind=kLoop, calls=%fused_computation.86 | loop fusion | flops 20971520 | bytes 24489984 | tf_op jit(solution)/shard_map/add | solution.py:43
  83.1 3.1 %collective-permute-start.6 = (f32[1,4,128,128]{3,2,1,0:T(8,128)S(1)}, f32[1,4,128,128]{3,2,1,0:T(8,128)S(1)}, u32[]{:S(2)}, u32[]{:S(2)}) collective-permute-start(f32[1,4,128,128]{3,2,1,0:T(8,128)S(1)} %get-tuple-element.27), channel_id=1, source_target_pairs={{0,16},{1,17},{2,18},{3,19},{4,20},{5,21},{6,22},{7,23},{8,24},{9,... | collective-permute-start | bytes 786440 | tf_op jit(solution)/shard_map/ppermute | solution.py:17
  87.4 2.6 collective-permute-done.6
  90.0 4.4 %collective-permute-done.7 = f32[1,4,128,128]{3,2,1,0:T(8,128)S(1)} collective-permute-done((f32[1,4,128,128]{3,2,1,0:T(8,128)S(1)}, f32[1,4,128,128]{3,2,1,0:T(8,128)S(1)}, u32[]{:S(2)}, u32[]{:S(2)}) %collective-permute-start.7) | collective-permute-done | bytes 262176 | tf_op jit(solution)/shard_map/ppermute | solution.py:19
  94.6 3.7 %collective-permute-start.8 = (f32[18,1,128,128]{3,2,1,0:T(8,128)S(1)}, f32[18,1,128,128]{3,2,1,0:T(8,128)S(1)}, u32[]{:S(2)}, u32[]{:S(2)}) collective-permute-start(f32[18,1,128,128]{3,2,1,0:T(8,128)S(1)} %get-tuple-element.19), channel_id=1, source_target_pairs={{0,4},{4,8},{8,12},{1,5},{5,9},{9,13},{2,6},{6,10},{10,14},{3,7},{... | collective-permute-start | bytes 3538952 | tf_op jit(solution)/shard_map/ppermute | solution.py:17
  99.6 19.0 %collective-permute-done.8 = f32[18,1,128,128]{3,2,1,0:T(8,128)S(1)} collective-permute-done((f32[18,1,128,128]{3,2,1,0:T(8,128)S(1)}, f32[18,1,128,128]{3,2,1,0:T(8,128)S(1)}, u32[]{:S(2)}, u32[]{:S(2)}) %collective-permute-start.8) | collective-permute-done | bytes 1179680 | tf_op jit(solution)/shard_map/ppermute | solution.py:17
  118.6 4.2 %collective-permute-done.9 = f32[18,1,128,128]{3,2,1,0:T(8,128)S(1)} collective-permute-done((f32[18,1,128,128]{3,2,1,0:T(8,128)S(1)}, f32[18,1,128,128]{3,2,1,0:T(8,128)S(1)}, u32[]{:S(2)}, u32[]{:S(2)}) %collective-permute-start.9) | collective-permute-done | bytes 1179680 | tf_op jit(solution)/shard_map/ppermute | solution.py:19
  126.6 4.3 %collective-permute-done.11 = f32[18,6,1,128]{3,2,1,0:T(1,128)S(1)} collective-permute-done((f32[18,6,1,128]{3,2,1,0:T(1,128)S(1)}, f32[18,6,1,128]{3,2,1,0:T(1,128)S(1)}, u32[]{:S(2)}, u32[]{:S(2)}) %collective-permute-start.11) | collective-permute-done | bytes 55328 | tf_op jit(solution)/shard_map/ppermute | solution.py:19
  130.8 5.5 %fusion.22 = f32[16,4,128,128]{3,2,1,0:T(8,128)S(1)} fusion(f32[16,4,128,128]{3,2,1,0:T(8,128)S(1)} %copy-done, f32[16,4,128,128]{3,2,1,0:T(8,128)S(1)} %fusion.31, f32[16,4,128,128]{3,2,1,0:T(8,128)S(1)} %copy-done.1, f32[18,6,1,128]{3,2,1,0:T(1,128)S(1)} %collective-permute-done.11, f32[18,1,128,128]{3,2,1,0:T(8,128)S(1)} %collective-permute-done.9, ...), kind=kLoop, calls=%fused_computation.59 | loop fusion | flops 29360128 | bytes 19771392 | tf_op jit(solution)/shard_map/add | solution.py:43
  139.4 2.6 collective-permute-done.12
  142.0 4.4 %collective-permute-done.13 = f32[1,4,128,128]{3,2,1,0:T(8,128)S(1)} collective-permute-done((f32[1,4,128,128]{3,2,1,0:T(8,128)S(1)}, f32[1,4,128,128]{3,2,1,0:T(8,128)S(1)}, u32[]{:S(2)}, u32[]{:S(2)}) %collective-permute-start.13) | collective-permute-done | bytes 262176 | tf_op jit(solution)/shard_map/ppermute | solution.py:19
  146.6 3.5 %collective-permute-start.14 = (f32[18,1,128,128]{3,2,1,0:T(8,128)S(1)}, f32[18,1,128,128]{3,2,1,0:T(8,128)S(1)}, u32[]{:S(2)}, u32[]{:S(2)}) collective-permute-start(f32[18,1,128,128]{3,2,1,0:T(8,128)S(1)} %get-tuple-element.17), channel_id=1, source_target_pairs={{0,4},{4,8},{8,12},{1,5},{5,9},{9,13},{2,6},{6,10},{10,14},{3,7},{... | collective-permute-start | bytes 3538952 | tf_op jit(solution)/shard_map/ppermute | solution.py:17
  151.4 15.6 %collective-permute-done.14 = f32[18,1,128,128]{3,2,1,0:T(8,128)S(1)} collective-permute-done((f32[18,1,128,128]{3,2,1,0:T(8,128)S(1)}, f32[18,1,128,128]{3,2,1,0:T(8,128)S(1)}, u32[]{:S(2)}, u32[]{:S(2)}) %collective-permute-start.14) | collective-permute-done | bytes 1179680 | tf_op jit(solution)/shard_map/ppermute | solution.py:17
  167.0 4.2 %collective-permute-done.15 = f32[18,1,128,128]{3,2,1,0:T(8,128)S(1)} collective-permute-done((f32[18,1,128,128]{3,2,1,0:T(8,128)S(1)}, f32[18,1,128,128]{3,2,1,0:T(8,128)S(1)}, u32[]{:S(2)}, u32[]{:S(2)}) %collective-permute-start.15) | collective-permute-done | bytes 1179680 | tf_op jit(solution)/shard_map/ppermute | solution.py:19
  174.9 4.3 %collective-permute-done.17 = f32[18,6,1,128]{3,2,1,0:T(1,128)S(1)} collective-permute-done((f32[18,6,1,128]{3,2,1,0:T(1,128)S(1)}, f32[18,6,1,128]{3,2,1,0:T(1,128)S(1)}, u32[]{:S(2)}, u32[]{:S(2)}) %collective-permute-start.17) | collective-permute-done | bytes 55328 | tf_op jit(solution)/shard_map/ppermute | solution.py:19
  179.2 5.7 %fusion.13 = f32[16,4,128,128]{3,2,1,0:T(8,128)S(1)} fusion(f32[16,4,128,128]{3,2,1,0:T(8,128)S(1)} %copy-done, f32[16,4,128,128]{3,2,1,0:T(8,128)S(1)} %fusion.22, f32[16,4,128,128]{3,2,1,0:T(8,128)S(1)} %copy-done.1, f32[18,6,1,128]{3,2,1,0:T(1,128)S(1)} %collective-permute-done.17, f32[18,1,128,128]{3,2,1,0:T(8,128)S(1)} %collective-permute-done.15, ...), kind=kLoop, calls=%fused_computation.32 | loop fusion | flops 29360128 | bytes 19771392 | tf_op jit(solution)/shard_map/add | solution.py:43
  188.0 2.6 collective-permute-done.18
  190.6 4.4 %collective-permute-done.19 = f32[1,4,128,128]{3,2,1,0:T(8,128)S(1)} collective-permute-done((f32[1,4,128,128]{3,2,1,0:T(8,128)S(1)}, f32[1,4,128,128]{3,2,1,0:T(8,128)S(1)}, u32[]{:S(2)}, u32[]{:S(2)}) %collective-permute-start.19) | collective-permute-done | bytes 262176 | tf_op jit(solution)/shard_map/ppermute | solution.py:19
  195.2 2.6 collective-permute-start.20
  199.1 12.7 %collective-permute-done.20 = f32[18,1,128,128]{3,2,1,0:T(8,128)S(1)} collective-permute-done((f32[18,1,128,128]{3,2,1,0:T(8,128)S(1)}, f32[18,1,128,128]{3,2,1,0:T(8,128)S(1)}, u32[]{:S(2)}, u32[]{:S(2)}) %collective-permute-start.20) | collective-permute-done | bytes 1179680 | tf_op jit(solution)/shard_map/ppermute | solution.py:17
  211.9 4.2 %collective-permute-done.21 = f32[18,1,128,128]{3,2,1,0:T(8,128)S(1)} collective-permute-done((f32[18,1,128,128]{3,2,1,0:T(8,128)S(1)}, f32[18,1,128,128]{3,2,1,0:T(8,128)S(1)}, u32[]{:S(2)}, u32[]{:S(2)}) %collective-permute-start.21) | collective-permute-done | bytes 1179680 | tf_op jit(solution)/shard_map/ppermute | solution.py:19
  219.5 4.3 %collective-permute-done.23 = f32[18,6,1,128]{3,2,1,0:T(1,128)S(1)} collective-permute-done((f32[18,6,1,128]{3,2,1,0:T(1,128)S(1)}, f32[18,6,1,128]{3,2,1,0:T(1,128)S(1)}, u32[]{:S(2)}, u32[]{:S(2)}) %collective-permute-start.23) | collective-permute-done | bytes 55328 | tf_op jit(solution)/shard_map/ppermute | solution.py:19
  223.8 7.5 %add_reduce_fusion = (f32[4,128,128]{2,1,0:T(8,128)}, f32[4,128,128]{2,1,0:T(8,128)}, f32[16,4,128,128]{3,2,1,0:T(8,128)}) fusion(f32[16,4,128,128]{3,2,1,0:T(8,128)S(1)} %copy-done, f32[16,4,128,128]{3,2,1,0:T(8,128)S(1)} %fusion.13, f32[16,4,128,128]{3,2,1,0:T(8,128)S(1)} %copy-done.1, f32[18,6,1,128]{3,2,1,0:T(1,128)S(1)} %collective-permute-done.23, ...), kind=kLoop, calls=%fused_computation.102 | loop fusion | flops 33423360 | bytes 20295680 | tf_op jit(solution)/shard_map/reduce_sum | solution.py:54
  231.4 25.1 %all-reduce.3.cloned.1.call-done = (f32[1,4,128,128]{3,2,1,0:T(8,128)}, f32[1,4,128,128]{3,2,1,0:T(8,128)}) async-done(((f32[1,4,128,128]{3,2,1,0:T(8,128)}, f32[1,4,128,128]{3,2,1,0:T(8,128)}), (f32[1,4,128,128]{3,2,1,0:T(8,128)}, f32[1,4,128,128]{3,2,1,0:T(8,128)})) %all-reduce.3.cloned.1.call-update) | async-done | bytes 524304 | tf_op jit(solution)/shard_map/psum | solution.py:53
  257.5 5.0 %subtract_multiply_fusion = f32[16,4,128,128]{3,2,1,0:T(8,128)} fusion(f32[16,4,128,128]{3,2,1,0:T(8,128)} %get-tuple-element.6, f32[4,128,128]{2,1,0:T(8,128)S(1)} %get-tuple-element.32, f32[4,128,128]{2,1,0:T(8,128)S(1)} %get-tuple-element.31), kind=kLoop, calls=%fused_computation.101 | loop fusion | flops 2097152 | bytes 8912896 | tf_op jit(solution)/shard_map/mul | solution.py:60
  (46 shorter events, 34.0 us)
Async XLA Ops:
  7.2 249.3 %all-reduce.3.cloned.1.call-start = ((), (), s32[]{:S(2)}) async-start(), calls=%async_computation | async-start | bytes 1048576 | tf_op jit(solution)/shard_map/psum | solution.py:53
  8.3 10.5 %collective-permute-start = (f32[1,4,128,128]{3,2,1,0:T(8,128)S(1)}, f32[1,4,128,128]{3,2,1,0:T(8,128)S(1)}, u32[]{:S(2)}, u32[]{:S(2)}) collective-permute-start(f32[1,4,128,128]{3,2,1,0:T(8,128)S(1)} %get-tuple-element.30), channel_id=1, source_target_pairs={{0,16},{1,17},{2,18},{3,19},{4,20},{5,21},{6,22},{7,23},{8,24},{9,... | collective-permute-start | bytes 786440 | tf_op jit(solution)/shard_map/ppermute | solution.py:17
  13.2 9.7 %collective-permute-start.1 = (f32[1,4,128,128]{3,2,1,0:T(8,128)S(1)}, f32[1,4,128,128]{3,2,1,0:T(8,128)S(1)}, u32[]{:S(2)}, u32[]{:S(2)}) collective-permute-start(f32[1,4,128,128]{3,2,1,0:T(8,128)S(1)} %get-tuple-element.29), channel_id=1, source_target_pairs={{16,0},{17,1},{18,2},{19,3},{20,4},{21,5},{22,6},{23,7},{24,8},{25... | collective-permute-start | bytes 786440 | tf_op jit(solution)/shard_map/ppermute | solution.py:19
  22.9 32.1 %copy-start.2 = (f32[18,4,128,128]{3,2,1,0:T(8,128)}, f32[18,4,128,128]{3,2,1,0:T(8,128)S(1)}, u32[]{:S(2)}) copy-start(f32[18,4,128,128]{3,2,1,0:T(8,128)S(1)} %constant_dynamic-update-slice_fusion) | copy-start | bytes 14155780
  23.1 27.6 %collective-permute-start.2 = (f32[18,1,128,128]{3,2,1,0:T(8,128)S(1)}, f32[18,1,128,128]{3,2,1,0:T(8,128)S(1)}, u32[]{:S(2)}, u32[]{:S(2)}) collective-permute-start(f32[18,1,128,128]{3,2,1,0:T(8,128)S(1)} %get-tuple-element.21), channel_id=1, source_target_pairs={{0,4},{4,8},{8,12},{1,5},{5,9},{9,13},{2,6},{6,10},{10,14},{3,7},{... | collective-permute-start | bytes 3538952 | tf_op jit(solution)/shard_map/ppermute | solution.py:17
  26.7 28.2 %collective-permute-start.3 = (f32[18,1,128,128]{3,2,1,0:T(8,128)S(1)}, f32[18,1,128,128]{3,2,1,0:T(8,128)S(1)}, u32[]{:S(2)}, u32[]{:S(2)}) collective-permute-start(f32[18,1,128,128]{3,2,1,0:T(8,128)S(1)} %get-tuple-element.22), channel_id=1, source_target_pairs={{4,0},{8,4},{12,8},{5,1},{9,5},{13,9},{6,2},{10,6},{14,10},{7,3},{... | collective-permute-start | bytes 3538952 | tf_op jit(solution)/shard_map/ppermute | solution.py:19
  55.0 5.2 %collective-permute-start.4 = (f32[18,6,1,128]{3,2,1,0:T(1,128)S(1)}, f32[18,6,1,128]{3,2,1,0:T(1,128)S(1)}, u32[]{:S(2)}, u32[]{:S(2)}) collective-permute-start(f32[18,6,1,128]{3,2,1,0:T(1,128)S(1)} %get-tuple-element.13), channel_id=1, source_target_pairs={{0,2},{1,3},{4,6},{5,7},{8,10},{9,11},{12,14},{13,15},{16,18},{17,... | collective-permute-start | bytes 165896 | tf_op jit(solution)/shard_map/ppermute | solution.py:17
  58.4 6.0 %collective-permute-start.5 = (f32[18,6,1,128]{3,2,1,0:T(1,128)S(1)}, f32[18,6,1,128]{3,2,1,0:T(1,128)S(1)}, u32[]{:S(2)}, u32[]{:S(2)}) collective-permute-start(f32[18,6,1,128]{3,2,1,0:T(1,128)S(1)} %get-tuple-element.14), channel_id=1, source_target_pairs={{2,0},{3,1},{6,4},{7,5},{10,8},{11,9},{14,12},{15,13},{18,16},{19,... | collective-permute-start | bytes 165896 | tf_op jit(solution)/shard_map/ppermute | solution.py:19
  83.1 6.9 %collective-permute-start.6 = (f32[1,4,128,128]{3,2,1,0:T(8,128)S(1)}, f32[1,4,128,128]{3,2,1,0:T(8,128)S(1)}, u32[]{:S(2)}, u32[]{:S(2)}) collective-permute-start(f32[1,4,128,128]{3,2,1,0:T(8,128)S(1)} %get-tuple-element.27), channel_id=1, source_target_pairs={{0,16},{1,17},{2,18},{3,19},{4,20},{5,21},{6,22},{7,23},{8,24},{9,... | collective-permute-start | bytes 786440 | tf_op jit(solution)/shard_map/ppermute | solution.py:17
  86.1 8.3 %collective-permute-start.7 = (f32[1,4,128,128]{3,2,1,0:T(8,128)S(1)}, f32[1,4,128,128]{3,2,1,0:T(8,128)S(1)}, u32[]{:S(2)}, u32[]{:S(2)}) collective-permute-start(f32[1,4,128,128]{3,2,1,0:T(8,128)S(1)} %get-tuple-element.28), channel_id=1, source_target_pairs={{16,0},{17,1},{18,2},{19,3},{20,4},{21,5},{22,6},{23,7},{24,8},{25... | collective-permute-start | bytes 786440 | tf_op jit(solution)/shard_map/ppermute | solution.py:19
  94.4 36.4 %copy-start.1 = (f32[16,4,128,128]{3,2,1,0:T(8,128)S(1)}, f32[16,4,128,128]{3,2,1,0:T(8,128)}, u32[]{:S(2)}) copy-start(f32[16,4,128,128]{3,2,1,0:T(8,128)} %param.4) | copy-start | bytes 12582916
  94.6 36.3 %copy-start = (f32[16,4,128,128]{3,2,1,0:T(8,128)S(1)}, f32[16,4,128,128]{3,2,1,0:T(8,128)}, u32[]{:S(2)}) copy-start(f32[16,4,128,128]{3,2,1,0:T(8,128)} %param.5) | copy-start | bytes 12582916
  94.6 24.0 %collective-permute-start.8 = (f32[18,1,128,128]{3,2,1,0:T(8,128)S(1)}, f32[18,1,128,128]{3,2,1,0:T(8,128)S(1)}, u32[]{:S(2)}, u32[]{:S(2)}) collective-permute-start(f32[18,1,128,128]{3,2,1,0:T(8,128)S(1)} %get-tuple-element.19), channel_id=1, source_target_pairs={{0,4},{4,8},{8,12},{1,5},{5,9},{9,13},{2,6},{6,10},{10,14},{3,7},{... | collective-permute-start | bytes 3538952 | tf_op jit(solution)/shard_map/ppermute | solution.py:17
  98.3 24.5 %collective-permute-start.9 = (f32[18,1,128,128]{3,2,1,0:T(8,128)S(1)}, f32[18,1,128,128]{3,2,1,0:T(8,128)S(1)}, u32[]{:S(2)}, u32[]{:S(2)}) collective-permute-start(f32[18,1,128,128]{3,2,1,0:T(8,128)S(1)} %get-tuple-element.20), channel_id=1, source_target_pairs={{4,0},{8,4},{12,8},{5,1},{9,5},{13,9},{6,2},{10,6},{14,10},{7,3},{... | collective-permute-start | bytes 3538952 | tf_op jit(solution)/shard_map/ppermute | solution.py:19
  122.9 3.7 %collective-permute-start.10 = (f32[18,6,1,128]{3,2,1,0:T(1,128)S(1)}, f32[18,6,1,128]{3,2,1,0:T(1,128)S(1)}, u32[]{:S(2)}, u32[]{:S(2)}) collective-permute-start(f32[18,6,1,128]{3,2,1,0:T(1,128)S(1)} %get-tuple-element.11), channel_id=1, source_target_pairs={{0,2},{1,3},{4,6},{5,7},{8,10},{9,11},{12,14},{13,15},{16,18},{17,... | collective-permute-start | bytes 165896 | tf_op jit(solution)/shard_map/ppermute | solution.py:17
  124.8 6.0 %collective-permute-start.11 = (f32[18,6,1,128]{3,2,1,0:T(1,128)S(1)}, f32[18,6,1,128]{3,2,1,0:T(1,128)S(1)}, u32[]{:S(2)}, u32[]{:S(2)}) collective-permute-start(f32[18,6,1,128]{3,2,1,0:T(1,128)S(1)} %get-tuple-element.12), channel_id=1, source_target_pairs={{2,0},{3,1},{6,4},{7,5},{10,8},{11,9},{14,12},{15,13},{18,16},{19,... | collective-permute-start | bytes 165896 | tf_op jit(solution)/shard_map/ppermute | solution.py:19
  136.3 5.6 %collective-permute-start.12 = (f32[1,4,128,128]{3,2,1,0:T(8,128)S(1)}, f32[1,4,128,128]{3,2,1,0:T(8,128)S(1)}, u32[]{:S(2)}, u32[]{:S(2)}) collective-permute-start(f32[1,4,128,128]{3,2,1,0:T(8,128)S(1)} %get-tuple-element.25), channel_id=1, source_target_pairs={{0,16},{1,17},{2,18},{3,19},{4,20},{5,21},{6,22},{7,23},{8,24},{9,... | collective-permute-start | bytes 786440 | tf_op jit(solution)/shard_map/ppermute | solution.py:17
  138.1 8.3 %collective-permute-start.13 = (f32[1,4,128,128]{3,2,1,0:T(8,128)S(1)}, f32[1,4,128,128]{3,2,1,0:T(8,128)S(1)}, u32[]{:S(2)}, u32[]{:S(2)}) collective-permute-start(f32[1,4,128,128]{3,2,1,0:T(8,128)S(1)} %get-tuple-element.26), channel_id=1, source_target_pairs={{16,0},{17,1},{18,2},{19,3},{20,4},{21,5},{22,6},{23,7},{24,8},{25... | collective-permute-start | bytes 786440 | tf_op jit(solution)/shard_map/ppermute | solution.py:19
  146.6 20.4 %collective-permute-start.14 = (f32[18,1,128,128]{3,2,1,0:T(8,128)S(1)}, f32[18,1,128,128]{3,2,1,0:T(8,128)S(1)}, u32[]{:S(2)}, u32[]{:S(2)}) collective-permute-start(f32[18,1,128,128]{3,2,1,0:T(8,128)S(1)} %get-tuple-element.17), channel_id=1, source_target_pairs={{0,4},{4,8},{8,12},{1,5},{5,9},{9,13},{2,6},{6,10},{10,14},{3,7},{... | collective-permute-start | bytes 3538952 | tf_op jit(solution)/shard_map/ppermute | solution.py:17
  150.1 21.1 %collective-permute-start.15 = (f32[18,1,128,128]{3,2,1,0:T(8,128)S(1)}, f32[18,1,128,128]{3,2,1,0:T(8,128)S(1)}, u32[]{:S(2)}, u32[]{:S(2)}) collective-permute-start(f32[18,1,128,128]{3,2,1,0:T(8,128)S(1)} %get-tuple-element.18), channel_id=1, source_target_pairs={{4,0},{8,4},{12,8},{5,1},{9,5},{13,9},{6,2},{10,6},{14,10},{7,3},{... | collective-permute-start | bytes 3538952 | tf_op jit(solution)/shard_map/ppermute | solution.py:19
  171.3 3.7 %collective-permute-start.16 = (f32[18,6,1,128]{3,2,1,0:T(1,128)S(1)}, f32[18,6,1,128]{3,2,1,0:T(1,128)S(1)}, u32[]{:S(2)}, u32[]{:S(2)}) collective-permute-start(f32[18,6,1,128]{3,2,1,0:T(1,128)S(1)} %get-tuple-element.9), channel_id=1, source_target_pairs={{0,2},{1,3},{4,6},{5,7},{8,10},{9,11},{12,14},{13,15},{16,18},{17,... | collective-permute-start | bytes 165896 | tf_op jit(solution)/shard_map/ppermute | solution.py:17
  173.2 6.0 %collective-permute-start.17 = (f32[18,6,1,128]{3,2,1,0:T(1,128)S(1)}, f32[18,6,1,128]{3,2,1,0:T(1,128)S(1)}, u32[]{:S(2)}, u32[]{:S(2)}) collective-permute-start(f32[18,6,1,128]{3,2,1,0:T(1,128)S(1)} %get-tuple-element.10), channel_id=1, source_target_pairs={{2,0},{3,1},{6,4},{7,5},{10,8},{11,9},{14,12},{15,13},{18,16},{19,... | collective-permute-start | bytes 165896 | tf_op jit(solution)/shard_map/ppermute | solution.py:19
  184.9 5.6 %collective-permute-start.18 = (f32[1,4,128,128]{3,2,1,0:T(8,128)S(1)}, f32[1,4,128,128]{3,2,1,0:T(8,128)S(1)}, u32[]{:S(2)}, u32[]{:S(2)}) collective-permute-start(f32[1,4,128,128]{3,2,1,0:T(8,128)S(1)} %get-tuple-element.23), channel_id=1, source_target_pairs={{0,16},{1,17},{2,18},{3,19},{4,20},{5,21},{6,22},{7,23},{8,24},{9,... | collective-permute-start | bytes 786440 | tf_op jit(solution)/shard_map/ppermute | solution.py:17
  186.7 8.3 %collective-permute-start.19 = (f32[1,4,128,128]{3,2,1,0:T(8,128)S(1)}, f32[1,4,128,128]{3,2,1,0:T(8,128)S(1)}, u32[]{:S(2)}, u32[]{:S(2)}) collective-permute-start(f32[1,4,128,128]{3,2,1,0:T(8,128)S(1)} %get-tuple-element.24), channel_id=1, source_target_pairs={{16,0},{17,1},{18,2},{19,3},{20,4},{21,5},{22,6},{23,7},{24,8},{25... | collective-permute-start | bytes 786440 | tf_op jit(solution)/shard_map/ppermute | solution.py:19
  195.2 16.7 %collective-permute-start.20 = (f32[18,1,128,128]{3,2,1,0:T(8,128)S(1)}, f32[18,1,128,128]{3,2,1,0:T(8,128)S(1)}, u32[]{:S(2)}, u32[]{:S(2)}) collective-permute-start(f32[18,1,128,128]{3,2,1,0:T(8,128)S(1)} %get-tuple-element.15), channel_id=1, source_target_pairs={{0,4},{4,8},{8,12},{1,5},{5,9},{9,13},{2,6},{6,10},{10,14},{3,7},{... | collective-permute-start | bytes 3538952 | tf_op jit(solution)/shard_map/ppermute | solution.py:17
  197.8 18.2 %collective-permute-start.21 = (f32[18,1,128,128]{3,2,1,0:T(8,128)S(1)}, f32[18,1,128,128]{3,2,1,0:T(8,128)S(1)}, u32[]{:S(2)}, u32[]{:S(2)}) collective-permute-start(f32[18,1,128,128]{3,2,1,0:T(8,128)S(1)} %get-tuple-element.16), channel_id=1, source_target_pairs={{4,0},{8,4},{12,8},{5,1},{9,5},{13,9},{6,2},{10,6},{14,10},{7,3},{... | collective-permute-start | bytes 3538952 | tf_op jit(solution)/shard_map/ppermute | solution.py:19
  216.2 3.4 %collective-permute-start.22 = (f32[18,6,1,128]{3,2,1,0:T(1,128)S(1)}, f32[18,6,1,128]{3,2,1,0:T(1,128)S(1)}, u32[]{:S(2)}, u32[]{:S(2)}) collective-permute-start(f32[18,6,1,128]{3,2,1,0:T(1,128)S(1)} %get-tuple-element.7), channel_id=1, source_target_pairs={{0,2},{1,3},{4,6},{5,7},{8,10},{9,11},{12,14},{13,15},{16,18},{17,... | collective-permute-start | bytes 165896 | tf_op jit(solution)/shard_map/ppermute | solution.py:17
  217.8 6.0 %collective-permute-start.23 = (f32[18,6,1,128]{3,2,1,0:T(1,128)S(1)}, f32[18,6,1,128]{3,2,1,0:T(1,128)S(1)}, u32[]{:S(2)}, u32[]{:S(2)}) collective-permute-start(f32[18,6,1,128]{3,2,1,0:T(1,128)S(1)} %get-tuple-element.8), channel_id=1, source_target_pairs={{2,0},{3,1},{6,4},{7,5},{10,8},{11,9},{14,12},{15,13},{18,16},{19,... | collective-permute-start | bytes 165896 | tf_op jit(solution)/shard_map/ppermute | solution.py:19
Sparse Core Ops, SparseCore 0:
  231.5 24.9 all-reduce.2
where the time goes:
time: 270 us; the launch traced here: 269 us
  waiting for transfers between devices  158 us (59%)
  starting transfers between devices  49.2 us (18%)
  other arithmetic  44.3 us (16%)
  between operations  14.4 us (5%)
  local copies, waits for them, and re-layouts  3.93 us (1%)
    ppermute x12, waiting for transfers between devices, extended(): lax.ppermute(tail, axis, [(i, (i + 1) % count) for i in range(ends)])  83.9 us
    ppermute x12, waiting for transfers between devices, extended(): lax.ppermute(head, axis, [((i + 1) % count, i) for i in range(ends)])  48.7 us
    ppermute x12, starting transfers between devices, extended(): lax.ppermute(tail, axis, [(i, (i + 1) % count) for i in range(ends)])  33.6 us
    add x3, other arithmetic, one_step(): return middle + conductance * spread + source  29.7 us
    psum x1, waiting for transfers between devices, on_device(): lax.psum((jnp.sum(moved, axis=0, keepdims=True), jnp.sum(moved * moved, a...  25.1 us
    ppermute x12, starting transfers between devices, extended(): lax.ppermute(head, axis, [((i + 1) % count, i) for i in range(ends)])  15.5 us
    reduce_sum x1, other arithmetic, on_device(): jnp.sum(moved, axis=0, keepdims=True)  7.53 us
  transfers between devices with their start and end apart: 25, of which 25 were waited for; matrix products, arithmetic and copies ran while one was open for 1% of the time, Pallas kernels for 0%

commit v1 on v0

v1 whole, which is shorter than its diff:
```python
import functools

import jax
import jax.numpy as jnp
from jax import lax
from jax.experimental import pallas as pl
from jax.experimental.pallas import tpu as pltpu
from jax.sharding import PartitionSpec as P

STEPS = 4
CHUNKS = 4
TILE = 8
MESH = pl.DeviceIdType.MESH


def kernel(
    sizes, chunks, field, conductance, source, anomaly, field_end,
    u, cond, src, last, scaled, own, others,
    load_sem, send_sem, recv_sem, ksend_sem, krecv_sem, ssend_sem, srecv_sem, out_sem,
):
    rows, cols, slabs = sizes
    nj, ni, nk, _ = field.shape
    kq = nk // chunks
    row, col, slab = (lax.axis_index(name) for name in ("rows", "cols", "slabs"))
    has = {
        "i-": col > 0, "i+": col < cols - 1,
        "j-": row > 0, "j+": row < rows - 1,
        "k-": slab > 0, "k+": slab < slabs - 1,
    }
    to = {
        "i-": {"cols": jnp.maximum(col - 1, 0)}, "i+": {"cols": jnp.minimum(col + 1, cols - 1)},
        "j-": {"rows": jnp.maximum(row - 1, 0)}, "j+": {"rows": jnp.minimum(row + 1, rows - 1)},
        "k-": {"slabs": jnp.maximum(slab - 1, 0)}, "k+": {"slabs": jnp.minimum(slab + 1, slabs - 1)},
    }
    opposite = {"i-": "i+", "i+": "i-", "j-": "j+", "j+": "j-", "k-": "k+", "k+": "k-"}
    sides = ("i-", "i+", "j-", "j+")
    descending = lax.rem(slab, 2) == 0

    loads = [
        pltpu.make_async_copy(field, u.at[0, pl.ds(1, nj), pl.ds(1, ni), pl.ds(TILE, nk)], load_sem.at[0]),
        pltpu.make_async_copy(conductance, cond, load_sem.at[1]),
        pltpu.make_async_copy(source, src, load_sem.at[2]),
    ]
    loads[0].start()

    barrier = pltpu.get_barrier_semaphore()
    expected = rows - 1
    for off in range(1, rows):
        pl.semaphore_signal(barrier, inc=1, device_id={"rows": lax.rem(row + off, rows)}, device_id_type=MESH)
    for side in ("i-", "i+", "k-", "k+"):
        expected = expected + jnp.where(has[side], 1, 0)

        @pl.when(has[side])
        def _():
            pl.semaphore_signal(barrier, inc=1, device_id=to[side], device_id_type=MESH)

    pl.semaphore_wait(barrier, expected)

    def chunk_of(n):
        return jnp.where(descending, chunks - 1 - n, n)

    def face(side, t, q, first):
        k0 = pl.multiple_of(q * kq, kq)
        inner = pl.ds(pl.multiple_of(TILE + k0, TILE), kq)
        js, is_ = pl.ds(1, nj), pl.ds(1, ni)
        if side[0] == "i":
            here, there = (1, ni + 1) if side == "i-" else (ni, 0)
            dst = u.at[t, js, there, inner]
            start = field.at[:, here - 1, pl.ds(k0, kq)] if first else u.at[t, js, here, inner]
        else:
            here, there = (1, nj + 1) if side == "j-" else (nj, 0)
            dst = u.at[t, there, is_, inner]
            start = field.at[here - 1, :, pl.ds(k0, kq)] if first else u.at[t, here, is_, inner]
        d = sides.index(side)
        return pltpu.make_async_remote_copy(
            src_ref=start, dst_ref=dst, send_sem=send_sem.at[d, t, q], recv_sem=recv_sem.at[d, t, q],
            device_id=to[side], device_id_type=MESH,
        )

    def kface(side, t, first):
        js, is_ = pl.ds(1, nj), pl.ds(1, ni)
        here, there = (TILE, TILE + nk) if side == "k-" else (nk, 0)
        start = field.at[:, :, pl.ds(here - TILE, TILE)] if first else u.at[t, js, is_, pl.ds(here, TILE)]
        d = 0 if side == "k-" else 1
        return pltpu.make_async_remote_copy(
            src_ref=start, dst_ref=u.at[t, js, is_, pl.ds(there, TILE)],
            send_sem=ksend_sem.at[d, t], recv_sem=krecv_sem.at[d, t],
            device_id=to[side], device_id_type=MESH,
        )

    def send_faces(t, q, first):
        for side in sides:
            @pl.when(has[side])
            def _():
                face(side, t, q, first).start()

        @pl.when((q == 0) & has["k-"])
        def _():
            kface("k-", t, first).start()

        @pl.when((q == chunks - 1) & has["k+"])
        def _():
            kface("k+", t, first).start()

    def wait_faces(t, q):
        for side in sides:
            @pl.when(has[opposite[side]])
            def _():
                face(side, t, q, False).wait_recv()

        @pl.when((q == chunks - 1) & has["k+"])
        def _():
            kface("k-", t, False).wait_recv()

        @pl.when((q == 0) & has["k-"])
        def _():
            kface("k+", t, False).wait_recv()

    @pl.loop(0, chunks)
    def _(n):
        send_faces(0, chunk_of(n), True)

    loads[1].start()
    loads[2].start()

    def zero_plane(t, j, i):
        u[t, j, i, pl.ds(TILE, nk)] = jnp.zeros((nk, u.shape[-1]), u.dtype)

    @pl.loop(0, STEPS)
    def _(t):
        for side, i in (("i-", 0), ("i+", ni + 1)):
            @pl.when(jnp.logical_not(has[side]))
            def _():
                @pl.loop(0, nj)
                def _(j):
                    zero_plane(t, j + 1, i)

        for side, j in (("j-", 0), ("j+", nj + 1)):
            @pl.when(jnp.logical_not(has[side]))
            def _():
                for i in range(ni):
                    zero_plane(t, j, i + 1)

        for side, k in (("k-", 0), ("k+", TILE + nk)):
            @pl.when(jnp.logical_not(has[side]))
            def _():
                @pl.loop(0, nj)
                def _(j):
                    for i in range(ni):
                        u[t, j + 1, i + 1, pl.ds(k, TILE)] = jnp.zeros((TILE, u.shape[-1]), u.dtype)

    for load in loads:
        load.wait()

    def stencil(t, j, i, k0):
        inner = pl.ds(pl.multiple_of(TILE + k0, TILE), kq)
        tall = u[t, j + 1, i + 1, pl.ds(k0, kq + 2 * TILE)]
        middle = tall[TILE:TILE + kq]
        spread = u[t, j, i + 1, inner] + u[t, j + 2, i + 1, inner]
        spread = spread + u[t, j + 1, i, inner] + u[t, j + 1, i + 2, inner]
        spread = spread + tall[TILE - 1:TILE - 1 + kq] + tall[TILE + 1:TILE + 1 + kq]
        spread = spread - 6.0 * middle
        own_k = pl.ds(k0, kq)
        return middle + cond[j, i, own_k] * spread + src[j, i, own_k]

    @pl.loop(0, (STEPS - 1) * chunks)
    def _(n):
        t = n // chunks
        q = chunk_of(lax.rem(n, chunks))
        k0 = pl.multiple_of(q * kq, kq)
        wait_faces(t, q)

        @pl.loop(0, nj)
        def _(jj):
            j = lax.rem(jj + nj - 1, nj)
            for i in range(ni):
                u[t + 1, j + 1, i + 1, pl.ds(pl.multiple_of(TILE + k0, TILE), kq)] = stencil(t, j, i, k0)

        send_faces(t + 1, q, False)

    def stats_copy(off, q):
        return pltpu.make_async_remote_copy(
            src_ref=own.at[q], dst_ref=others.at[off - 1, q],
            send_sem=ssend_sem.at[off - 1, q], recv_sem=srecv_sem.at[off - 1, q],
            device_id={"rows": lax.rem(row + off, rows)}, device_id_type=MESH,
        )

    def out_copy(which, q):
        ks = pl.ds(pl.multiple_of(q * kq, kq), kq)
        start, dst = ((last, field_end), (scaled, anomaly))[which]
        return pltpu.make_async_copy(start.at[:, :, ks], dst.at[:, :, ks], out_sem.at[which, q])

    def final_step(n):
        q = chunk_of(n)
        k0 = pl.multiple_of(q * kq, kq)
        ks = pl.ds(k0, kq)
        wait_faces(STEPS - 1, q)

        def step(j, totals):
            sums = []
            for i in range(ni):
                new = stencil(STEPS - 1, j, i, k0)
                last[j, i, ks] = new
                sums.append(totals[i] + new)
            return tuple(sums)

        zero = jnp.zeros((kq, u.shape[-1]), u.dtype)
        totals = lax.fori_loop(0, nj, step, (zero,) * ni)
        for i in range(ni):
            mean = totals[i] / nj
            own[q, 0, i] = mean

            def spread_of(j, total):
                away = last[j, i, ks] - mean
                return total + away * away

            own[q, 1, i] = lax.fori_loop(0, nj, spread_of, zero)
        out_copy(0, q).start()
        for off in range(1, rows):
            stats_copy(off, q).start()

    def finish(n):
        q = chunk_of(n)
        ks = pl.ds(pl.multiple_of(q * kq, kq), kq)
        for off in range(1, rows):
            stats_copy(off, q).wait_recv()
        for i in range(ni):
            means = [own[q, 0, i]] + [others[off - 1, q, 0, i] for off in range(1, rows)]
            spreads = [own[q, 1, i]] + [others[off - 1, q, 1, i] for off in range(1, rows)]
            mean = sum(means[1:], means[0]) / rows
            spread = sum(spreads[1:], spreads[0])
            for other in means:
                spread = spread + nj * ((other - mean) * (other - mean))
            scale = lax.rsqrt(spread / (nj * rows) + 0.0001)

            @pl.loop(0, nj)
            def _(j):
                scaled[j, i, ks] = (last[j, i, ks] - mean) * scale
        out_copy(1, q).start()

    @pl.loop(0, chunks)
    def _(n):
        final_step(n)

        @pl.when(n > 0)
        def _():
            finish(n - 1)

    finish(chunks - 1)

    @pl.loop(0, STEPS * chunks)
    def _(n):
        for side in sides:
            @pl.when(has[side])
            def _():
                face(side, n // chunks, lax.rem(n, chunks), False).wait_send()

    @pl.loop(0, STEPS)
    def _(t):
        for side in ("k-", "k+"):
            @pl.when(has[side])
            def _():
                kface(side, t, False).wait_send()

    @pl.loop(0, chunks)
    def _(q):
        for off in range(1, rows):
            stats_copy(off, q).wait_send()
        out_copy(0, q).wait()
        out_copy(1, q).wait()


def on_device(field_values, conductance, source):
    sizes = tuple(lax.axis_size(name) for name in ("rows", "cols", "slabs"))
    nj, ni, nk, levels = field_values.shape
    chunks = CHUNKS if nk % (CHUNKS * TILE) == 0 else 1
    kq = nk // chunks
    peers = max(sizes[0] - 1, 1)
    whole = jax.ShapeDtypeStruct(field_values.shape, field_values.dtype)
    anywhere = pl.BlockSpec(memory_space=pl.ANY)
    return pl.pallas_call(
        functools.partial(kernel, sizes, chunks),
        out_shape=(whole, whole),
        in_specs=[anywhere] * 3,
        out_specs=(anywhere, anywhere),
        scratch_shapes=[
            pltpu.VMEM((STEPS, nj + 2, ni + 2, nk + 2 * TILE, levels), jnp.float32),
            pltpu.VMEM((nj, ni, nk, levels), jnp.float32),
            pltpu.VMEM((nj, ni, nk, levels), jnp.float32),
            pltpu.VMEM((nj, ni, nk, levels), jnp.float32),
            pltpu.VMEM((nj, ni, nk, levels), jnp.float32),
            pltpu.VMEM((chunks, 2, ni, kq, levels), jnp.float32),
            pltpu.VMEM((peers, chunks, 2, ni, kq, levels), jnp.float32),
            pltpu.SemaphoreType.DMA((3,)),
            pltpu.SemaphoreType.DMA((4, STEPS, chunks)),
            pltpu.SemaphoreType.DMA((4, STEPS, chunks)),
            pltpu.SemaphoreType.DMA((2, STEPS)),
            pltpu.SemaphoreType.DMA((2, STEPS)),
            pltpu.SemaphoreType.DMA((peers, chunks)),
            pltpu.SemaphoreType.DMA((peers, chunks)),
            pltpu.SemaphoreType.DMA((2, chunks)),
        ],
        compiler_params=pltpu.CompilerParams(
            collective_id=0, has_side_effects=True, vmem_limit_bytes=64 * 1024 * 1024 - 65536
        ),
        name="heat_steps",
    )(field_values, conductance, source)


def solution(mesh):
    spec = P(("trial", "rows"), "cols", "slabs", None)
    return jax.shard_map(
        on_device, mesh=mesh, in_specs=(spec,) * 3, out_specs=(spec, spec), check_vma=False
    )
```

time: 270 us -> 111 us (0.41)
  waiting for transfers between devices: 158 us -> 0 us
  Pallas kernels: 0 us -> 104 us
  starting transfers between devices: 49.2 us -> 0 us
  other arithmetic: 44.3 us -> 0 us
  between operations: 14.4 us -> 0.65 us
  local copies, waits for them, and re-layouts: 3.93 us -> 6.87 us
    ppermute x24 -> x0, waiting for transfers between devices: 133 us -> none  [the longest x12 83.9 us: extended(): lax.ppermute(tail, axis, [(i, (i + 1) % count) for i in range(ends)])]
    pallas_call x0 -> x1, Pallas kernels: none -> 104 us  [on_device(): pl.pallas_call(functools.partial(kernel, sizes, chunks), out_shape=(whole...]
    ppermute x24 -> x0, starting transfers between devices: 49.2 us -> none  [the longest x12 33.6 us: extended(): lax.ppermute(tail, axis, [(i, (i + 1) % count) for i in range(ends)])]
    add x3 -> x0, other arithmetic: 29.7 us -> none  [one_step(): return middle + conductance * spread + source]
    psum x1 -> x0, waiting for transfers between devices: 25.1 us -> none  [on_device(): lax.psum((jnp.sum(moved, axis=0, keepdims=True), jnp.sum(moved * moved, a...]
    reduce_sum x1 -> x0, other arithmetic: 7.53 us -> none  [on_device(): jnp.sum(moved, axis=0, keepdims=True)]
    mul x1 -> x0, other arithmetic: 4.99 us -> none  [on_device(): anomaly = centred * lax.rsqrt(line_variance + 0.0001)]
    unnamed x8 -> x4, local copies, waits for them, and re-layouts: 2.5 us -> 6.87 us
  transfers between devices with their start and end apart: 25 -> 0, of which waited for: 25 -> 0; matrix products, arithmetic and copies ran while one was open for 1% -> 0% of each run, Pallas kernels for 0% -> 0%
where the time goes in v1:
time: 111 us
  Pallas kernels  104 us (94%)
  local copies, waits for them, and re-layouts  6.87 us (6%)
    pallas_call x1, Pallas kernels, on_device(): pl.pallas_call(functools.partial(kernel, sizes, chunks), out_shape=(whole...  104 us
    unnamed x4, local copies, waits for them, and re-layouts  6.87 us

profile of v1, /device:TPU:0, one launch (start us, length us, event | category | flops | bytes accessed | tf_op | source)
XLA Modules:
  0.0 111.2 jit_solution(13689161420913184611)
XLA Ops:
  0.6 103.7 %heat_steps.1 = (f32[16,4,128,128]{3,2,1,0:T(8,128)}, f32[16,4,128,128]{3,2,1,0:T(8,128)}) custom-call(f32[16,4,128,128]{3,2,1,0:T(8,128)} %field.1, f32[16,4,128,128]{3,2,1,0:T(8,128)} %conductance.1, f32[16,4,128,128]{3,2,1,0:T(8,128)} %source.1), custom_call_target="tpu_custom_call" | custom-call | tf_op jit(solution)/shard_map/heat_steps/pallas_call | solution.py:281
  104.3 0.0 copy-start
  104.3 4.8 %copy.7 = f32[16,4,128,128]{3,2,1,0:T(8,128)} copy(f32[16,4,128,128]{3,2,1,0:T(8,128)} %get-tuple-element.4) | data formatting | bytes 8388608
  109.2 0.0 copy-done
  109.2 2.0 %copy.8 = f32[16,4,128,128]{3,2,1,0:T(8,128)} copy(f32[16,4,128,128]{3,2,1,0:T(8,128)S(1)} %copy-done) | data formatting | bytes 8388608
Async XLA Ops:
  104.3 4.9 %copy-start = (f32[16,4,128,128]{3,2,1,0:T(8,128)S(1)}, f32[16,4,128,128]{3,2,1,0:T(8,128)}, u32[]{:S(2)}) copy-start(f32[16,4,128,128]{3,2,1,0:T(8,128)} %get-tuple-element.5) | copy-start | bytes 12582916

commit v2 on v1

--- a/solution.py
+++ b/solution.py
@@ -8,15 +8,15 @@
 from jax.sharding import PartitionSpec as P
 
 STEPS = 4
-CHUNKS = 4
+CHUNKS = 8
 TILE = 8
 MESH = pl.DeviceIdType.MESH
 
 
 def kernel(
-    sizes, chunks, field, conductance, source, anomaly, field_end,
-    u, cond, src, last, scaled, own, others,
-    load_sem, send_sem, recv_sem, ksend_sem, krecv_sem, ssend_sem, srecv_sem, out_sem,
+    sizes, chunks, field, conductance, source, scaled, last,
+    u, cond, src, own, others,
+    load_sem, send_sem, recv_sem, ksend_sem, krecv_sem, ssend_sem, srecv_sem,
 ):
     rows, cols, slabs = sizes
     nj, ni, nk, _ = field.shape
@@ -185,11 +185,6 @@
             device_id={"rows": lax.rem(row + off, rows)}, device_id_type=MESH,
         )
 
-    def out_copy(which, q):
-        ks = pl.ds(pl.multiple_of(q * kq, kq), kq)
-        start, dst = ((last, field_end), (scaled, anomaly))[which]
-        return pltpu.make_async_copy(start.at[:, :, ks], dst.at[:, :, ks], out_sem.at[which, q])
-
     def final_step(n):
         q = chunk_of(n)
         k0 = pl.multiple_of(q * kq, kq)
@@ -215,7 +210,6 @@
                 return total + away * away
 
             own[q, 1, i] = lax.fori_loop(0, nj, spread_of, zero)
-        out_copy(0, q).start()
         for off in range(1, rows):
             stats_copy(off, q).start()
 
@@ -236,7 +230,6 @@
             @pl.loop(0, nj)
             def _(j):
                 scaled[j, i, ks] = (last[j, i, ks] - mean) * scale
-        out_copy(1, q).start()
 
     @pl.loop(0, chunks)
     def _(n):
@@ -266,8 +259,6 @@
     def _(q):
         for off in range(1, rows):
             stats_copy(off, q).wait_send()
-        out_copy(0, q).wait()
-        out_copy(1, q).wait()
 
 
 def on_device(field_values, conductance, source):
@@ -276,17 +267,16 @@
     chunks = CHUNKS if nk % (CHUNKS * TILE) == 0 else 1
     kq = nk // chunks
     peers = max(sizes[0] - 1, 1)
-    whole = jax.ShapeDtypeStruct(field_values.shape, field_values.dtype)
+    whole = pltpu.VMEM(field_values.shape, field_values.dtype)
+    near = pl.BlockSpec(memory_space=pltpu.VMEM)
     anywhere = pl.BlockSpec(memory_space=pl.ANY)
     return pl.pallas_call(
         functools.partial(kernel, sizes, chunks),
         out_shape=(whole, whole),
         in_specs=[anywhere] * 3,
-        out_specs=(anywhere, anywhere),
+        out_specs=(near, near),
         scratch_shapes=[
             pltpu.VMEM((STEPS, nj + 2, ni + 2, nk + 2 * TILE, levels), jnp.float32),
-            pltpu.VMEM((nj, ni, nk, levels), jnp.float32),
-            pltpu.VMEM((nj, ni, nk, levels), jnp.float32),
             pltpu.VMEM((nj, ni, nk, levels), jnp.float32),
             pltpu.VMEM((nj, ni, nk, levels), jnp.float32),
             pltpu.VMEM((chunks, 2, ni, kq, levels), jnp.float32),
@@ -298,10 +288,9 @@
             pltpu.SemaphoreType.DMA((2, STEPS)),
             pltpu.SemaphoreType.DMA((peers, chunks)),
             pltpu.SemaphoreType.DMA((peers, chunks)),
-            pltpu.SemaphoreType.DMA((2, chunks)),
         ],
         compiler_params=pltpu.CompilerParams(
-            collective_id=0, has_side_effects=True, vmem_limit_bytes=64 * 1024 * 1024 - 65536
+            collective_id=0, has_side_effects=True, vmem_limit_bytes=52 * 1024 * 1024
         ),
         name="heat_steps",
     )(field_values, conductance, source)

time: 111 us -> 109 us (0.982)
  local copies, waits for them, and re-layouts: 6.87 us -> 4.03 us
    unnamed x4 -> x2, local copies, waits for them, and re-layouts: 6.87 us -> 4.03 us
where the time goes in v2:
time: 109 us
  Pallas kernels  104 us (95%)
  local copies, waits for them, and re-layouts  4.03 us (4%)
    pallas_call x1, Pallas kernels, on_device(): pl.pallas_call(functools.partial(kernel, sizes, chunks), out_shape=(whole...  104 us
    unnamed x2, local copies, waits for them, and re-layouts  4.03 us

profile of v2, /device:TPU:0, one launch (start us, length us, event | category | flops | bytes accessed | tf_op | source)
XLA Modules:
  0.0 108.7 jit_solution(15109716079270846633)
XLA Ops:
  0.6 104.0 %heat_steps.1 = (f32[16,4,128,128]{3,2,1,0:T(8,128)S(1)}, f32[16,4,128,128]{3,2,1,0:T(8,128)S(1)}) custom-call(f32[16,4,128,128]{3,2,1,0:T(8,128)} %field.1, f32[16,4,128,128]{3,2,1,0:T(8,128)} %conductance.1, f32[16,4,128,128]{3,2,1,0:T(8,128)} %source.1), custom_call_target="tpu_custom_call" | custom-call | tf_op jit(solution)/shard_map/heat_steps/pallas_call | solution.py:273
  104.6 2.0 %copy.7 = f32[16,4,128,128]{3,2,1,0:T(8,128)} copy(f32[16,4,128,128]{3,2,1,0:T(8,128)S(1)} %get-tuple-element.2) | data formatting | bytes 8388608
  106.7 2.0 %copy.8 = f32[16,4,128,128]{3,2,1,0:T(8,128)} copy(f32[16,4,128,128]{3,2,1,0:T(8,128)S(1)} %get-tuple-element.3) | data formatting | bytes 8388608

commit v3 on v2

--- a/solution.py
+++ b/solution.py
@@ -8,19 +8,18 @@
 from jax.sharding import PartitionSpec as P
 
 STEPS = 4
-CHUNKS = 8
 TILE = 8
+PIECES = 4
 MESH = pl.DeviceIdType.MESH
 
 
 def kernel(
-    sizes, chunks, field, conductance, source, scaled, last,
+    sizes, parts, field, conductance, source, scaled, last,
     u, cond, src, own, others,
     load_sem, send_sem, recv_sem, ksend_sem, krecv_sem, ssend_sem, srecv_sem,
 ):
     rows, cols, slabs = sizes
     nj, ni, nk, _ = field.shape
-    kq = nk // chunks
     row, col, slab = (lax.axis_index(name) for name in ("rows", "cols", "slabs"))
     has = {
         "i-": col > 0, "i+": col < cols - 1,
@@ -56,11 +55,18 @@
 
     pl.semaphore_wait(barrier, expected)
 
-    def chunk_of(n):
-        return jnp.where(descending, chunks - 1 - n, n)
-
-    def face(side, t, q, first):
-        k0 = pl.multiple_of(q * kq, kq)
+    def start_of(t, n):
+        before, size = sum(parts[t][:n]), parts[t][n]
+        return pl.multiple_of(jnp.where(descending, nk - before - size, before), TILE)
+
+    def edges_of(t, n):
+        first, final = n == 0, n == len(parts[t]) - 1
+        low = jnp.where(descending, final, first)
+        high = jnp.where(descending, first, final)
+        return low, high
+
+    def face(side, t, n, first):
+        k0, kq = start_of(t, n), parts[t][n]
         inner = pl.ds(pl.multiple_of(TILE + k0, TILE), kq)
         js, is_ = pl.ds(1, nj), pl.ds(1, ni)
         if side[0] == "i":
@@ -73,7 +79,7 @@
             start = field.at[here - 1, :, pl.ds(k0, kq)] if first else u.at[t, here, is_, inner]
         d = sides.index(side)
         return pltpu.make_async_remote_copy(
-            src_ref=start, dst_ref=dst, send_sem=send_sem.at[d, t, q], recv_sem=recv_sem.at[d, t, q],
+            src_ref=start, dst_ref=dst, send_sem=send_sem.at[d, t, n], recv_sem=recv_sem.at[d, t, n],
             device_id=to[side], device_id_type=MESH,
         )
 
@@ -88,37 +94,38 @@
             device_id=to[side], device_id_type=MESH,
         )
 
-    def send_faces(t, q, first):
+    def send_faces(t, n, first):
+        low, high = edges_of(t, n)
         for side in sides:
             @pl.when(has[side])
             def _():
-                face(side, t, q, first).start()
-
-        @pl.when((q == 0) & has["k-"])
+                face(side, t, n, first).start()
+
+        @pl.when(low & has["k-"])
         def _():
             kface("k-", t, first).start()
 
-        @pl.when((q == chunks - 1) & has["k+"])
+        @pl.when(high & has["k+"])
         def _():
             kface("k+", t, first).start()
 
-    def wait_faces(t, q):
+    def wait_faces(t, n):
+        low, high = edges_of(t, n)
         for side in sides:
             @pl.when(has[opposite[side]])
             def _():
-                face(side, t, q, False).wait_recv()
-
-        @pl.when((q == chunks - 1) & has["k+"])
+                face(side, t, n, False).wait_recv()
+
+        @pl.when(high & has["k+"])
         def _():
             kface("k-", t, False).wait_recv()
 
-        @pl.when((q == 0) & has["k-"])
+        @pl.when(low & has["k-"])
         def _():
             kface("k+", t, False).wait_recv()
 
-    @pl.loop(0, chunks)
-    def _(n):
-        send_faces(0, chunk_of(n), True)
+    for n in range(len(parts[0])):
+        send_faces(0, n, True)
 
     loads[1].start()
     loads[2].start()
@@ -152,7 +159,7 @@
     for load in loads:
         load.wait()
 
-    def stencil(t, j, i, k0):
+    def stencil(t, j, i, k0, kq):
         inner = pl.ds(pl.multiple_of(TILE + k0, TILE), kq)
         tall = u[t, j + 1, i + 1, pl.ds(k0, kq + 2 * TILE)]
         middle = tall[TILE:TILE + kq]
@@ -163,64 +170,65 @@
         own_k = pl.ds(k0, kq)
         return middle + cond[j, i, own_k] * spread + src[j, i, own_k]
 
-    @pl.loop(0, (STEPS - 1) * chunks)
-    def _(n):
-        t = n // chunks
-        q = chunk_of(lax.rem(n, chunks))
-        k0 = pl.multiple_of(q * kq, kq)
-        wait_faces(t, q)
+    def middle_step(t, n):
+        k0, kq = start_of(t, n), parts[t][n]
+        wait_faces(t, n)
 
         @pl.loop(0, nj)
         def _(jj):
             j = lax.rem(jj + nj - 1, nj)
             for i in range(ni):
-                u[t + 1, j + 1, i + 1, pl.ds(pl.multiple_of(TILE + k0, TILE), kq)] = stencil(t, j, i, k0)
-
-        send_faces(t + 1, q, False)
-
-    def stats_copy(off, q):
+                u[t + 1, j + 1, i + 1, pl.ds(pl.multiple_of(TILE + k0, TILE), kq)] = stencil(t, j, i, k0, kq)
+
+        low, done = sum(parts[t][:n]), sum(parts[t][:n + 1])
+        for m in range(len(parts[t + 1])):
+            if low <= sum(parts[t + 1][:m]) < done:
+                send_faces(t + 1, m, False)
+
+    for t in range(STEPS - 1):
+        for n in range(len(parts[t])):
+            middle_step(t, n)
+
+    final = parts[STEPS - 1]
+
+    def span_of(n):
+        return pl.ds(start_of(STEPS - 1, n), final[n])
+
+    def stats_copy(off, n):
         return pltpu.make_async_remote_copy(
-            src_ref=own.at[q], dst_ref=others.at[off - 1, q],
-            send_sem=ssend_sem.at[off - 1, q], recv_sem=srecv_sem.at[off - 1, q],
+            src_ref=own.at[:, :, span_of(n)], dst_ref=others.at[off - 1, :, :, span_of(n)],
+            send_sem=ssend_sem.at[off - 1, n], recv_sem=srecv_sem.at[off - 1, n],
             device_id={"rows": lax.rem(row + off, rows)}, device_id_type=MESH,
         )
 
     def final_step(n):
-        q = chunk_of(n)
-        k0 = pl.multiple_of(q * kq, kq)
-        ks = pl.ds(k0, kq)
-        wait_faces(STEPS - 1, q)
-
-        def step(j, totals):
-            sums = []
-            for i in range(ni):
-                new = stencil(STEPS - 1, j, i, k0)
+        k0, kq, ks = start_of(STEPS - 1, n), final[n], span_of(n)
+        wait_faces(STEPS - 1, n)
+        zero = jnp.zeros((kq, u.shape[-1]), u.dtype)
+        for i in range(ni):
+            def step(j, total):
+                new = stencil(STEPS - 1, j, i, k0, kq)
                 last[j, i, ks] = new
-                sums.append(totals[i] + new)
-            return tuple(sums)
-
-        zero = jnp.zeros((kq, u.shape[-1]), u.dtype)
-        totals = lax.fori_loop(0, nj, step, (zero,) * ni)
-        for i in range(ni):
-            mean = totals[i] / nj
-            own[q, 0, i] = mean
+                return total + new
+
+            mean = lax.fori_loop(0, nj, step, zero, unroll=2) / nj
+            own[0, i, ks] = mean
 
             def spread_of(j, total):
                 away = last[j, i, ks] - mean
                 return total + away * away
 
-            own[q, 1, i] = lax.fori_loop(0, nj, spread_of, zero)
+            own[1, i, ks] = lax.fori_loop(0, nj, spread_of, zero, unroll=2)
         for off in range(1, rows):
-            stats_copy(off, q).start()
+            stats_copy(off, n).start()
 
     def finish(n):
-        q = chunk_of(n)
-        ks = pl.ds(pl.multiple_of(q * kq, kq), kq)
+        ks = span_of(n)
         for off in range(1, rows):
-            stats_copy(off, q).wait_recv()
+            stats_copy(off, n).wait_recv()
         for i in range(ni):
-            means = [own[q, 0, i]] + [others[off - 1, q, 0, i] for off in range(1, rows)]
-            spreads = [own[q, 1, i]] + [others[off - 1, q, 1, i] for off in range(1, rows)]
+            means = [own[0, i, ks]] + [others[off - 1, 0, i, ks] for off in range(1, rows)]
+            spreads = [own[1, i, ks]] + [others[off - 1, 1, i, ks] for off in range(1, rows)]
             mean = sum(means[1:], means[0]) / rows
             spread = sum(spreads[1:], spreads[0])
             for other in means:
@@ -231,47 +239,62 @@
             def _(j):
                 scaled[j, i, ks] = (last[j, i, ks] - mean) * scale
 
-    @pl.loop(0, chunks)
-    def _(n):
+    for n in range(len(final)):
         final_step(n)
-
-        @pl.when(n > 0)
-        def _():
+        if n > 0:
             finish(n - 1)
-
-    finish(chunks - 1)
-
-    @pl.loop(0, STEPS * chunks)
-    def _(n):
+    finish(len(final) - 1)
+
+    for t in range(STEPS):
         for side in sides:
             @pl.when(has[side])
             def _():
-                face(side, n // chunks, lax.rem(n, chunks), False).wait_send()
-
-    @pl.loop(0, STEPS)
-    def _(t):
+                for n in range(len(parts[t])):
+                    face(side, t, n, False).wait_send()
+
         for side in ("k-", "k+"):
             @pl.when(has[side])
             def _():
                 kface(side, t, False).wait_send()
 
-    @pl.loop(0, chunks)
-    def _(q):
+    for n in range(len(final)):
         for off in range(1, rows):
-            stats_copy(off, q).wait_send()
+            stats_copy(off, n).wait_send()
+
+
+def write_out(near_anomaly, near_field, anomaly, field_end, sems):
+    copies = []
+    for which, (start, dst) in enumerate(((near_field, field_end), (near_anomaly, anomaly))):
+        pieces = sems.shape[1]
+        depth = start.shape[0] // pieces
+        for piece in range(pieces):
+            js = pl.ds(piece * depth, depth)
+            copies.append(pltpu.make_async_copy(start.at[js], dst.at[js], sems.at[which, piece]))
+    for copy in copies:
+        copy.start()
+    for copy in copies:
+        copy.wait()
+
+
+def parts_of(nk):
+    half = nk // 2 if nk % (2 * TILE) == 0 else nk
+    coarse = (half,) * (nk // half)
+    small = half * 3 // 8 // TILE * TILE
+    fine = coarse[:-1] + ((half - small, small) if small else (half,))
+    return (coarse,) * (STEPS - 1) + (fine,)
 
 
 def on_device(field_values, conductance, source):
     sizes = tuple(lax.axis_size(name) for name in ("rows", "cols", "slabs"))
     nj, ni, nk, levels = field_values.shape
-    chunks = CHUNKS if nk % (CHUNKS * TILE) == 0 else 1
-    kq = nk // chunks
+    parts = parts_of(nk)
+    most = max(len(of) for of in parts)
     peers = max(sizes[0] - 1, 1)
     whole = pltpu.VMEM(field_values.shape, field_values.dtype)
     near = pl.BlockSpec(memory_space=pltpu.VMEM)
     anywhere = pl.BlockSpec(memory_space=pl.ANY)
-    return pl.pallas_call(
-        functools.partial(kernel, sizes, chunks),
+    results = pl.pallas_call(
+        functools.partial(kernel, sizes, parts),
         out_shape=(whole, whole),
         in_specs=[anywhere] * 3,
         out_specs=(near, near),
@@ -279,21 +302,32 @@
             pltpu.VMEM((STEPS, nj + 2, ni + 2, nk + 2 * TILE, levels), jnp.float32),
             pltpu.VMEM((nj, ni, nk, levels), jnp.float32),
             pltpu.VMEM((nj, ni, nk, levels), jnp.float32),
-            pltpu.VMEM((chunks, 2, ni, kq, levels), jnp.float32),
-            pltpu.VMEM((peers, chunks, 2, ni, kq, levels), jnp.float32),
+            pltpu.VMEM((2, ni, nk, levels), jnp.float32),
+            pltpu.VMEM((peers, 2, ni, nk, levels), jnp.float32),
             pltpu.SemaphoreType.DMA((3,)),
-            pltpu.SemaphoreType.DMA((4, STEPS, chunks)),
-            pltpu.SemaphoreType.DMA((4, STEPS, chunks)),
+            pltpu.SemaphoreType.DMA((4, STEPS, most)),
+            pltpu.SemaphoreType.DMA((4, STEPS, most)),
             pltpu.SemaphoreType.DMA((2, STEPS)),
             pltpu.SemaphoreType.DMA((2, STEPS)),
-            pltpu.SemaphoreType.DMA((peers, chunks)),
-            pltpu.SemaphoreType.DMA((peers, chunks)),
+            pltpu.SemaphoreType.DMA((peers, most)),
+            pltpu.SemaphoreType.DMA((peers, most)),
         ],
         compiler_params=pltpu.CompilerParams(
             collective_id=0, has_side_effects=True, vmem_limit_bytes=52 * 1024 * 1024
         ),
         name="heat_steps",
     )(field_values, conductance, source)
+    there = jax.ShapeDtypeStruct(field_values.shape, field_values.dtype)
+    pieces = PIECES if nj % PIECES == 0 else 1
+    return pl.pallas_call(
+        write_out,
+        out_shape=(there, there),
+        in_specs=[near] * 2,
+        out_specs=(anywhere, anywhere),
+        scratch_shapes=[pltpu.SemaphoreType.DMA((2, pieces))],
+        compiler_params=pltpu.CompilerParams(vmem_limit_bytes=1024 * 1024),
+        name="write_out",
+    )(*results)
 
 
 def solution(mesh):

time: 109 us -> 106 us (0.972)
  local copies, waits for them, and re-layouts: 4.03 us -> 0 us
    unnamed x2 -> x0, local copies, waits for them, and re-layouts: 4.03 us -> none
    pallas_call x1 -> x2, Pallas kernels: 104 us -> 105 us  [the longest x1 102 us: on_device(): pl.pallas_call(functools.partial(kernel, sizes, parts), out_shape=(whole,...]
where the time goes in v3:
time: 106 us
  Pallas kernels  105 us (99%)
    pallas_call x1, Pallas kernels, on_device(): pl.pallas_call(functools.partial(kernel, sizes, parts), out_shape=(whole,...  102 us
    pallas_call x1, Pallas kernels, on_device(): pl.pallas_call(write_out, out_shape=(there, there), in_specs=[near] * 2,...  3.37 us

profile of v3, /device:TPU:0, one launch (start us, length us, event | category | flops | bytes accessed | tf_op | source)
XLA Modules:
  0.0 106.0 jit_solution(3824230407495583549)
XLA Ops:
  0.6 102.0 %heat_steps.1 = (f32[16,4,128,128]{3,2,1,0:T(8,128)S(1)}, f32[16,4,128,128]{3,2,1,0:T(8,128)S(1)}) custom-call(f32[16,4,128,128]{3,2,1,0:T(8,128)} %field.1, f32[16,4,128,128]{3,2,1,0:T(8,128)} %conductance.1, f32[16,4,128,128]{3,2,1,0:T(8,128)} %source.1), custom_call_target="tpu_custom_call" | custom-call | tf_op jit(solution)/shard_map/heat_steps/pallas_call | solution.py:296
  102.6 3.4 %write_out.1 = (f32[16,4,128,128]{3,2,1,0:T(8,128)}, f32[16,4,128,128]{3,2,1,0:T(8,128)}) custom-call(f32[16,4,128,128]{3,2,1,0:T(8,128)S(1)} %get-tuple-element.4.near_anomaly, f32[16,4,128,128]{3,2,1,0:T(8,128)S(1)} %get-tuple-element.5.near_field), custom_call_target="tpu_custom_call" | custom-call | tf_op jit(solution)/shard_map/write_out/pallas_call | solution.py:322
